TPU v7x, 32 devices: a whole 2x2x4 slice. The times are simulated.
32 devices in a mesh: rep: 4 (over x, y), dp: 8 (over z, core).
Axes of the slice: x: 2, y: 2, z: 4, core: 2. Of those that a mesh axis runs over, the one named last changes fastest.
Arguments:
- g_w_gate: bfloat16 [32, 2, 1536, 4224], P(('rep', 'dp')), parts along dimension 0
- g_w_up: bfloat16 [32, 2, 1536, 4224], P(('rep', 'dp')), parts along dimension 0
- g_w_down: bfloat16 [32, 2, 4224, 1536], P(('rep', 'dp')), parts along dimension 0
- w_gate: bfloat16 [2, 1536, 4224], replicated
- w_up: bfloat16 [2, 1536, 4224], replicated
- w_down: bfloat16 [2, 4224, 1536], replicated
- m_w_gate: float32 [2, 1536, 4224], P(None, 'dp')
- m_w_up: float32 [2, 1536, 4224], P(None, 'dp')
- m_w_down: float32 [2, 4224, 1536], P(None, 'dp')
- v_w_gate: float32 [2, 1536, 4224], P(None, 'dp')
- v_w_up: float32 [2, 1536, 4224], P(None, 'dp')
- v_w_down: float32 [2, 4224, 1536], P(None, 'dp')
Outputs:
- output 1: bfloat16 [8, 1536, 4224], P('rep'), parts along dimension 0
- output 2: bfloat16 [8, 1536, 4224], P('rep'), parts along dimension 0
- output 3: bfloat16 [8, 4224, 1536], P('rep'), parts along dimension 0
- output 4: float32 [8, 1536, 4224], P('rep', 'dp'), parts along dimension 0
- output 5: float32 [8, 1536, 4224], P('rep', 'dp'), parts along dimension 0
- output 6: float32 [8, 4224, 1536], P('rep', 'dp'), parts along dimension 0
- output 7: float32 [8, 1536, 4224], P('rep', 'dp'), parts along dimension 0
- output 8: float32 [8, 1536, 4224], P('rep', 'dp'), parts along dimension 0
- output 9: float32 [8, 4224, 1536], P('rep', 'dp'), parts along dimension 0
There are 4 independent parts. A program takes and returns all parts, laid end to end along the dimension named above; an argument that names none is the same for every part.
All inputs are finite; a program needn't handle non-finite values.
Results may differ from a plain program's by a relative error of at most 0.022.
Values are sent between devices in bfloat16 or wider.
A program may use at most 2 GiB of HBM per device.

v0:
```python
import jax
import jax.numpy as jnp
from jax import lax
from jax.sharding import PartitionSpec as P


def adamw(w, m, v, g):
    m = 0.9 * m + 0.1 * g
    v = 0.95 * v + 0.05 * g * g
    step = m * lax.rsqrt(v + 1e-8) + 0.1 * w
    return (w - 0.02 * step).astype(jnp.bfloat16), m, v


def clipped(gradients, sum_of_squares, count):
    factor = jnp.minimum(1.0, 0.5 * lax.rsqrt(sum_of_squares / count + 1e-30))
    return [g * factor for g in gradients]


def solution(mesh):
    def step(*arrays):
        terms, weights, m, v = (arrays[i : i + 3] for i in (0, 3, 6, 9))
        gradients = [lax.psum_scatter(t[0], "dp", scatter_dimension=1, tiled=True).astype(jnp.float32) for t in terms]
        squares = lax.psum(sum(jnp.sum(g * g) for g in gradients), "dp")
        gradients = clipped(gradients, squares, lax.psum(1, "dp") * sum(g.size for g in gradients))
        me = lax.axis_index("dp")
        own = [lax.dynamic_slice_in_dim(w, me * one.shape[1], one.shape[1], 1).astype(jnp.float32) for w, one in zip(weights, m, strict=True)]
        new = [adamw(w, m, v, g) for w, m, v, g in zip(own, m, v, gradients, strict=True)]
        whole = [lax.all_gather(one[0], "dp", axis=1, tiled=True) for one in new]
        return (*whole, *(one[1] for one in new), *(one[2] for one in new))

    all_of, cut = P(None, None, None), P(None, "dp", None)
    return jax.shard_map(
        step,
        mesh=mesh,
        in_specs=(P(("rep", "dp"), None, None, None),) * 3 + (all_of,) * 3 + (cut,) * 6,
        out_specs=(P("rep", None, None),) * 3 + (P("rep", "dp", None),) * 6,
        check_vma=False,
    )
```

profile of v0, /device:TPU:0, one launch (start us, length us, event | category | flops | bytes accessed | tf_op | source)
XLA Modules:
  0.0 1554.4 jit_solution(12791890440266494678)
XLA Ops:
  7.2 0.0 reduce-scatter.4.cloned.1.call-start
  7.2 0.7 reduce-scatter.4.cloned.1.call-update
  7.9 0.0 reduce-scatter.6.cloned.1.call-start
  8.0 0.7 reduce-scatter.6.cloned.1.call-update
  8.7 0.0 reduce-scatter.8.cloned.1.call-start
  8.7 0.7 reduce-scatter.8.cloned.1.call-update
  9.4 0.0 all-gather.8.cloned.1.call-start
  9.4 258.0 %reduce-scatter.4.cloned.1.call-done = bf16[2,192,4224]{2,1,0:T(8,128)(2,1)} async-done(((bf16[2,1536,4224]{2,1,0:T(8,128)(2,1)}), bf16[2,192,4224]{2,1,0:T(8,128)(2,1)}) %reduce-scatter.4.cloned.1.call-update) | async-done | bytes 3244048 | tf_op jit(solution)/shard_map/reduce_scatter | solution.py:22
  267.4 4.2 fusion.9
  271.6 251.2 %reduce-scatter.6.cloned.1.call-done = bf16[2,192,4224]{2,1,0:T(8,128)(2,1)} async-done(((bf16[2,1536,4224]{2,1,0:T(8,128)(2,1)}), bf16[2,192,4224]{2,1,0:T(8,128)(2,1)}) %reduce-scatter.6.cloned.1.call-update) | async-done | bytes 3244048 | tf_op jit(solution)/shard_map/reduce_scatter | solution.py:22
  522.9 4.2 fusion.10
  528.4 249.9 %reduce-scatter.8.cloned.1.call-done = bf16[2,528,1536]{2,1,0:T(8,128)(2,1)} async-done(((bf16[2,4224,1536]{2,1,0:T(8,128)(2,1)}), bf16[2,528,1536]{2,1,0:T(8,128)(2,1)}) %reduce-scatter.8.cloned.1.call-update) | async-done | bytes 3244048 | tf_op jit(solution)/shard_map/reduce_scatter | solution.py:22
  778.3 4.2 fusion.11
  783.1 14.3 psum.7
  798.2 13.1 fusion.17
  811.3 0.0 all-gather.8.cloned.1.call-update
  811.3 0.0 all-gather.4.cloned.1.call-start
  811.4 0.0 copy-start
  811.4 13.6 fusion.8
  825.0 0.0 all-gather.4.cloned.1.call-update
  825.0 0.0 all-gather.6.cloned.1.call-start
  825.1 0.0 copy-done
  825.1 11.4 fusion.14
  836.5 0.0 all-gather.6.cloned.1.call-update
  836.5 200.1 %all-gather.8.cloned.1.call-done = bf16[2,4224,1536]{2,1,0:T(8,128)(2,1)} async-done(((bf16[2,528,1536]{2,1,0:T(8,128)(2,1)}), bf16[2,4224,1536]{2,1,0:T(8,128)(2,1)}) %all-gather.8.cloned.1.call-update) | async-done | bytes 25952272 | tf_op jit(solution)/shard_map/all_gather | solution.py:28
  1036.7 227.6 %all-gather.4.cloned.1.call-done = bf16[2,1536,4224]{2,1,0:T(8,128)(2,1)} async-done(((bf16[2,192,4224]{2,1,0:T(8,128)(2,1)}), bf16[2,1536,4224]{2,1,0:T(8,128)(2,1)}) %all-gather.4.cloned.1.call-update) | async-done | bytes 25952272 | tf_op jit(solution)/shard_map/all_gather | solution.py:28
  1264.3 227.6 %all-gather.6.cloned.1.call-done = bf16[2,1536,4224]{2,1,0:T(8,128)(2,1)} async-done(((bf16[2,192,4224]{2,1,0:T(8,128)(2,1)}), bf16[2,1536,4224]{2,1,0:T(8,128)(2,1)}) %all-gather.6.cloned.1.call-update) | async-done | bytes 25952272 | tf_op jit(solution)/shard_map/all_gather | solution.py:28
  1491.9 0.0 slice-start
  1491.9 0.0 slice-start.1
  1491.9 0.0 slice-start.2
  1491.9 0.0 slice-start.3
  1491.9 23.8 %copy.24 = bf16[2,1536,4224]{2,1,0:T(8,128)(2,1)} copy(bf16[2,1536,4224]{2,1,0:T(8,128)(2,1)} %all-gather.4.cloned.1.call-done) | data formatting | bytes 51904512
  1515.8 0.0 slice-start.4
  1515.8 0.0 slice-start.5
  1515.8 0.0 slice-start.6
  1515.8 22.6 %copy.25 = bf16[2,1536,4224]{2,1,0:T(8,128)(2,1)} copy(bf16[2,1536,4224]{2,1,0:T(8,128)(2,1)} %all-gather.6.cloned.1.call-done) | data formatting | bytes 51904512
  1538.3 0.0 slice-done
  1538.3 0.0 slice-done.1
  1538.3 0.0 slice-done.2
  1538.3 0.0 slice-done.3
  1538.4 0.0 slice-done.4
  1538.4 0.0 slice-done.5
  1538.4 0.0 slice-done.6
  1538.4 9.2 copy.26
  (1 shorter events, 0.0 us)
Async XLA Ops:
  7.2 260.3 %reduce-scatter.4.cloned.1.call-start = ((), (), s32[]{:S(2)}) async-start(), calls=%async_computation.3 | async-start | bytes 29196288 | tf_op jit(solution)/shard_map/reduce_scatter | solution.py:22
  7.9 515.0 %reduce-scatter.6.cloned.1.call-start = ((), (), s32[]{:S(2)}) async-start(), calls=%async_computation.4 | async-start | bytes 29196288 | tf_op jit(solution)/shard_map/reduce_scatter | solution.py:22
  8.7 769.6 %reduce-scatter.8.cloned.1.call-start = ((), (), s32[]{:S(2)}) async-start(), calls=%async_computation.5 | async-start | bytes 29196288 | tf_op jit(solution)/shard_map/reduce_scatter | solution.py:22
  9.4 1027.3 %all-gather.8.cloned.1.call-start = ((), (), s32[]{:S(2)}) async-start(), calls=%async_computation.8 | async-start | bytes 29196288 | tf_op jit(solution)/shard_map/all_gather | solution.py:28
  811.3 452.9 %all-gather.4.cloned.1.call-start = ((), (), s32[]{:S(2)}) async-start(), calls=%async_computation.6 | async-start | bytes 29196288 | tf_op jit(solution)/shard_map/all_gather | solution.py:28
  811.4 13.7 copy-start
  825.0 666.9 %all-gather.6.cloned.1.call-start = ((), (), s32[]{:S(2)}) async-start(), calls=%async_computation.7 | async-start | bytes 29196288 | tf_op jit(solution)/shard_map/all_gather | solution.py:28
  1491.9 46.4 %slice-start = ((s8[25952256]{0:T(1024)(128)(4,1)}), s8[4194304]{0:T(1024)(128)(4,1)S(1)}, s32[]{:S(2)}) async-start(s8[25952256]{0:T(1024)(128)(4,1)} %bitcast.6), calls=%async_computation.9 | async-start | bytes 8388608
  1491.9 46.4 %slice-start.1 = ((s8[25952256]{0:T(1024)(128)(4,1)}), s8[4194304]{0:T(1024)(128)(4,1)S(1)}, s32[]{:S(2)}) async-start(s8[25952256]{0:T(1024)(128)(4,1)} %bitcast.6), calls=%async_computation.10 | async-start | bytes 8388608
  1491.9 46.4 %slice-start.2 = ((s8[25952256]{0:T(1024)(128)(4,1)}), s8[4194304]{0:T(1024)(128)(4,1)S(1)}, s32[]{:S(2)}) async-start(s8[25952256]{0:T(1024)(128)(4,1)} %bitcast.6), calls=%async_computation.11 | async-start | bytes 8388608
  1491.9 46.4 %slice-start.3 = ((s8[25952256]{0:T(1024)(128)(4,1)}), s8[4194304]{0:T(1024)(128)(4,1)S(1)}, s32[]{:S(2)}) async-start(s8[25952256]{0:T(1024)(128)(4,1)} %bitcast.6), calls=%async_computation.12 | async-start | bytes 8388608
  1515.8 22.6 %slice-start.4 = ((s8[25952256]{0:T(1024)(128)(4,1)}), s8[4194304]{0:T(1024)(128)(4,1)S(1)}, s32[]{:S(2)}) async-start(s8[25952256]{0:T(1024)(128)(4,1)} %bitcast.6), calls=%async_computation.13 | async-start | bytes 8388608
  1515.8 22.6 %slice-start.5 = ((s8[25952256]{0:T(1024)(128)(4,1)}), s8[4194304]{0:T(1024)(128)(4,1)S(1)}, s32[]{:S(2)}) async-start(s8[25952256]{0:T(1024)(128)(4,1)} %bitcast.6), calls=%async_computation.14 | async-start | bytes 8388608
  1515.8 22.6 %slice-start.6 = ((s8[25952256]{0:T(1024)(128)(4,1)}), s8[786432]{0:T(1024)(128)(4,1)S(1)}, s32[]{:S(2)}) async-start(s8[25952256]{0:T(1024)(128)(4,1)} %bitcast.6), calls=%async_computation.15 | async-start | bytes 1572864
Sparse Core Ops, SparseCore 0:
  10.4 257.0 reduce-scatter.3
  269.8 253.0 reduce-scatter.5
  525.3 253.0 reduce-scatter.7
  811.5 225.1 all-gather.7
  1038.7 225.5 all-gather.3
  1266.3 225.5 all-gather.5
where the time goes:
time: 1550 us
  waiting for transfers between devices  1420 us (92%)
  local copies, waits for them, and re-layouts  55.6 us (4%)
  other arithmetic  50.7 us (3%)
  between operations  16.8 us (1%)
    reduce_scatter x3, waiting for transfers between devices, step(): lax.psum_scatter(t[0], 'dp', scatter_dimension=1, tiled=True)  759 us
    all_gather x3, waiting for transfers between devices, step(): whole = [lax.all_gather(one[0], 'dp', axis=1, tiled=True) for one in new]  655 us
    unnamed x19, local copies, waits for them, and re-layouts  55.6 us
    convert_element_type x3, other arithmetic, adamw(): return ((w - 0.02 * step).astype(jnp.bfloat16), m, v)  38.2 us
  transfers between devices with their start and end apart: 6, of which 6 were waited for; matrix products, arithmetic and copies ran while one was open for 2% of the time, Pallas kernels for 0%

commit v1 on v0

v1 whole, which is shorter than its diff:
```python
import functools

import jax
import jax.numpy as jnp
from jax import lax
from jax.experimental import pallas as pl
from jax.experimental.pallas import tpu as pltpu
from jax.sharding import PartitionSpec as P

MESH = pl.DeviceIdType.MESH
ANY = pl.BlockSpec(memory_space=pl.ANY)
BF16, F32 = jnp.bfloat16, jnp.float32
PIECES = 3
PER_WEIGHT = 2 * PIECES
PER_BLOCK = 3 * PER_WEIGHT
SLOTS = 3
GROUP = 16


def place():
    rep, dp = lax.axis_index("rep"), lax.axis_index("dp")
    chip, core = dp // 2, lax.rem(dp, 2)
    low = chip < 2
    end = jnp.logical_or(chip == 0, chip == 3)

    def at(near, other=False):
        z = jnp.where(low, near, 3 - near)
        return 2 * z + (1 - core if other else core)

    return rep, dp, end, at


def piece(q):
    return q // PIECES, lax.rem(q, PIECES)


def rows_of(block, height, q, rows):
    return pl.ds(pl.multiple_of(block * height + lax.rem(q, PIECES) * rows, 16), rows)


def remote(src, dst, send, recv, device):
    return pltpu.make_async_remote_copy(src_ref=src, dst_ref=dst, send_sem=send, recv_sem=recv, device_id=device, device_id_type=MESH)


def add_up(rows, ins, out, acc=None):
    @pl.loop(0, rows // GROUP)
    def _(i):
        at = pl.ds(pl.multiple_of(i * GROUP, GROUP), GROUP)
        total = ins[0][at, :].astype(F32)
        for one in ins[1:]:
            total = total + one[at, :].astype(F32)
        rounded = total.astype(BF16)
        out[at, :] = rounded
        if acc is not None:
            g = rounded.astype(F32)
            acc[...] += g * g


def reduce_kernel(heights, *refs):
    terms, m, v = refs[0:3], refs[3:6], refs[6:9]
    g, g_near, m_near, v_near, from_side, from_half, from_core = (refs[9 + 3 * i : 12 + 3 * i] for i in range(7))
    squares = refs[30]
    scratch = refs[31:]
    inward, outward = scratch[0:2], scratch[2:4]
    loads = scratch[4:6]
    acc = scratch[6:8]
    gathered = scratch[8]
    in_send, out_send, load_sem, store_sem, side_sem, half_sem, core_send, core_recv, mv_send, mv_recv, rel_send, rel_recv, sq_send, sq_recv = scratch[9:]
    rep, dp, end, at = place()
    partner = (rep, at(jnp.where(end, 0, 1), True))
    side = (rep, at(jnp.where(end, 1, 0)))
    half = (rep, at(2))
    rows = [h // PIECES for h in heights]
    kind = (0, 0, 1)

    def core_copy(near, w, layer):
        block = at(near, True)
        n = (near * 3 + w) * 2 + layer
        src = terms[w].at[0, layer, pl.ds(pl.multiple_of(block * heights[w], 16), heights[w]), :]
        return remote(src, from_core[w].at[near, layer], core_send.at[n], core_recv.at[n], partner)

    def mv_copies(w, do_send_sem, do_recv_sem, src_pair, device, quarter, base):
        part = heights[w] // 2
        cut = (quarter // 2, pl.ds(pl.multiple_of(lax.rem(quarter, 2) * part, 8), part))
        out = []
        for i, (src, dst) in enumerate(zip(src_pair, (m_near[w], v_near[w]), strict=True)):
            n = base + 2 * w + i
            out.append(remote(src.at[cut], dst.at[cut], do_send_sem.at[n], do_recv_sem.at[n], device))
        return out

    def relay(w, hop):
        peer = (lax.rem(rep + hop, 4), dp)
        return mv_copies(w, rel_send, rel_recv, (m_near[w], v_near[w]), peer, rep, 6 * (hop - 1))

    def load(w, slot, near, q, ins):
        layer, _ = piece(q)
        sources = [terms[w].at[0, layer, rows_of(at(near), heights[w], q, rows[w]), :]]
        sources += [r.at[layer, rows_of(0, heights[w], q, rows[w]), :] for r in (from_core[w].at[near], *ins)]
        copies = [pltpu.make_async_copy(s, loads[kind[w]].at[slot, i], load_sem.at[slot, i]) for i, s in enumerate(sources)]
        for c in copies:
            c.start()
        return copies

    def into(w, slot, n):
        return [loads[kind[w]].at[slot, i] for i in range(n)]

    def wait_core(near, w, q):
        @pl.when(lax.rem(q, PIECES) == 0)
        def _():
            core_copy(near, w, q // PIECES).wait_recv()

    def side_landing(near, w, q, where):
        layer, _ = piece(q)
        return where.at[layer, rows_of(0, heights[w], q, rows[w]), :]

    def send(w, stage, n, slot, sems, where, q, recv, device):
        return remote(stage[kind[w]].at[slot], side_landing(0, w, q, where), sems.at[kind[w], slot], recv.at[n], device)

    def arrived(w, q, where, recv, n):
        ref = side_landing(0, w, q, where)
        remote(ref, ref, in_send.at[0, 0], recv.at[n], side).wait_recv()

    def reuse(w, q, first, stage, sems, where, recv, device):
        @pl.when(jnp.logical_or(q >= SLOTS, jnp.logical_not(first)))
        def _():
            send(w, stage, 0, lax.rem(q, SLOTS), sems, where, q, recv, device).wait_send()

    acc[0][...] = jnp.zeros_like(acc[0])
    acc[1][...] = jnp.zeros_like(acc[1])

    @pl.when(end)
    def _():
        for near in (3, 2, 1, 0):
            for w in range(3):
                for layer in range(2):
                    core_copy(near, w, layer).start()

    @pl.when(jnp.logical_not(end))
    def _():
        for near in (3, 2, 0, 1):
            for w in range(3):
                for layer in range(2):
                    core_copy(near, w, layer).start()
        for w in range(3):
            for c in mv_copies(w, mv_send, mv_recv, (m[w], v[w]), side, rep, 0):
                c.start()

    @pl.when(end)
    def _():
        for phase, near in enumerate((3, 2, 1)):
            for w in range(3):
                fresh = phase == 0 and w in (0, 2)
                for back in (w - 1,) if phase == 0 else ((2,) if phase == 1 and w == 0 else ()):
                    if back >= 0:
                        for c in mv_copies(back, mv_send, mv_recv, (m_near[back], v_near[back]), side, rep, 0):
                            c.wait_recv()
                        for hop in (1, 2, 3):
                            for c in relay(back, hop):
                                c.start()

                @pl.loop(0, PER_WEIGHT)
                def _(q, w=w, phase=phase, near=near, fresh=fresh):
                    slot = lax.rem(q, SLOTS)
                    wait_core(near, w, q)
                    copies = load(w, 0, near, q, ())
                    own = []
                    if phase == 2:
                        wait_core(0, w, q)
                        arrived(w, q, from_side[w].at[0], side_sem, w * PER_WEIGHT + q)
                        own = load(w, 1, 0, q, (from_side[w].at[0],))
                    reuse(w, q, fresh, inward, in_send, from_side[w].at[phase], side_sem, side)
                    for c in copies:
                        c.wait()
                    add_up(rows[w], into(w, 0, 2), inward[kind[w]].at[slot])
                    send(w, inward, phase * PER_BLOCK + w * PER_WEIGHT + q, slot, in_send, from_side[w].at[phase], q, side_sem, side).start()
                    if phase == 2:
                        layer, _ = piece(q)
                        for c in own:
                            c.wait()
                        out = outward[kind[w]].at[slot]
                        add_up(rows[w], into(w, 1, 3), out, acc[kind[w]])
                        store = pltpu.make_async_copy(out, g[w].at[layer, rows_of(0, heights[w], q, rows[w]), :], store_sem)
                        store.start()
                        store.wait()

        for k in range(2):
            w = (0, 2)[k]
            for slot in range(SLOTS):
                send(w, inward, 0, slot, in_send, from_side[w].at[2], 0, side_sem, side).wait_send()
        for w in range(3):

            @pl.loop(0, PER_WEIGHT)
            def _(q, w=w):
                arrived(w, q, g_near[w], side_sem, PER_BLOCK + w * PER_WEIGHT + q)

            for hop in (1, 2, 3):
                for c in relay(w, hop):
                    c.wait_send()
                source = lax.rem(rep + 4 - hop, 4)
                for c in mv_copies(w, rel_send, rel_recv, (m_near[w], v_near[w]), partner, source, 6 * (hop - 1)):
                    c.wait_recv()

    @pl.when(jnp.logical_not(end))
    def _():
        for phase, near in enumerate((3, 2, 1)):
            for w in range(3):
                fresh = phase == 0 and w in (0, 2)
                fresh_out = phase == 1 and w in (0, 2)

                @pl.loop(0, PER_WEIGHT)
                def _(q, w=w, phase=phase, near=near, fresh=fresh, fresh_out=fresh_out):
                    slot = lax.rem(q, SLOTS)
                    layer, _ = piece(q)
                    n = w * PER_WEIGHT + q
                    if phase == 1:
                        wait_core(0, w, q)
                        arrived(w, q, from_half[w].at[0], half_sem, n)
                        own = load(w, 1, 0, q, (from_half[w].at[0],))
                    wait_core(near, w, q)
                    arrived(w, q, from_side[w].at[phase], side_sem, phase * PER_BLOCK + n)
                    if phase < 2:
                        copies = load(w, 0, near, q, (from_side[w].at[phase],))
                        reuse(w, q, fresh, inward, in_send, from_half[w].at[phase], half_sem, half)
                        for c in copies:
                            c.wait()
                        add_up(rows[w], into(w, 0, 3), inward[kind[w]].at[slot])
                        send(w, inward, phase * PER_BLOCK + n, slot, in_send, from_half[w].at[phase], q, half_sem, half).start()
                        if phase == 1:
                            reuse(w, q, fresh_out, outward, out_send, from_side[w].at[0], side_sem, side)
                            for c in own:
                                c.wait()
                            add_up(rows[w], into(w, 1, 3), outward[kind[w]].at[slot])
                            send(w, outward, n, slot, out_send, from_side[w].at[0], q, side_sem, side).start()
                    else:
                        arrived(w, q, from_half[w].at[1], half_sem, PER_BLOCK + n)
                        copies = load(w, 0, near, q, (from_side[w].at[2], from_half[w].at[1]))
                        reuse(w, q, False, outward, out_send, g_near[w], side_sem, side)
                        for c in copies:
                            c.wait()
                        out = outward[kind[w]].at[slot]
                        add_up(rows[w], into(w, 0, 4), out, acc[kind[w]])
                        send(w, outward, PER_BLOCK + n, slot, out_send, g_near[w], q, side_sem, side).start()
                        store = pltpu.make_async_copy(out, g[w].at[layer, rows_of(0, heights[w], q, rows[w]), :], store_sem)
                        store.start()
                        store.wait()

        for k in range(2):
            w = (0, 2)[k]
            for slot in range(SLOTS):
                send(w, inward, 0, slot, in_send, from_half[w].at[1], 0, half_sem, half).wait_send()
                send(w, outward, 0, slot, out_send, g_near[w], 0, side_sem, side).wait_send()
        for w in range(3):
            for c in mv_copies(w, mv_send, mv_recv, (m[w], v[w]), side, rep, 0):
                c.wait_send()

    for near in range(4):
        for w in range(3):
            for layer in range(2):
                core_copy(near, w, layer).wait_send()

    tile = jnp.zeros((GROUP, 128), F32)
    for one in acc:
        for j in range(one.shape[1] // 128):
            tile = tile + one[:, j * 128 : (j + 1) * 128]
    gathered[dp] = tile
    for hop in range(1, 8):
        to = lax.rem(dp + hop, 8)
        remote(gathered.at[dp], gathered.at[dp], sq_send.at[hop - 1], sq_recv.at[hop - 1], (rep, to)).start()
    for hop in range(1, 8):
        source = lax.rem(dp + 8 - hop, 8)
        c = remote(gathered.at[source], gathered.at[source], sq_send.at[hop - 1], sq_recv.at[hop - 1], (rep, lax.rem(dp + hop, 8)))
        c.wait_send()
        c.wait_recv()
    squares[...] = gathered[...]


def gather_kernel(heights, *refs):
    factor, new, w_old, g_near, m_near, v_near = refs[0], *(refs[1 + 3 * i : 4 + 3 * i] for i in range(5))
    whole = refs[16:19]
    scratch = refs[19:]
    g_in, w_in, m_in, v_in, out = (scratch[2 * i : 2 * i + 2] for i in range(5))
    load_sem, store_sem, ici_send, core_send, side_sem, half_sem, core_recv = scratch[10:]
    rep, dp, end, at = place()
    me = jnp.where(end, 0, 1)
    partner = (rep, at(me, True))
    side = (rep, at(1 - me))
    half = (rep, at(2))
    rows = [h // PIECES for h in heights]
    kind = (0, 0, 1)

    def spot(w, near, q, other=False):
        return whole[w].at[q // PIECES, rows_of(at(near, other), heights[w], q, rows[w]), :]

    def own(w, q):
        return new[w].at[q // PIECES, rows_of(0, heights[w], q, rows[w]), :]

    def to_core(w, near, q, src):
        n = near * PER_BLOCK + w * PER_WEIGHT + q
        return remote(src, spot(w, near, q), core_send.at[n], core_recv.at[n], partner)

    def from_core(w, near, q):
        n = near * PER_BLOCK + w * PER_WEIGHT + q
        ref = spot(w, near, q, True)
        remote(ref, ref, core_send.at[n], core_recv.at[n], partner).wait_recv()

    def to_side(w, near, q, which, src):
        n = which * PER_BLOCK + w * PER_WEIGHT + q
        return remote(src, spot(w, near, q), ici_send.at[n], side_sem.at[n], side)

    def to_half(w, near, q, which, src):
        n = which * PER_BLOCK + w * PER_WEIGHT + q
        return remote(src, spot(w, near, q), ici_send.at[2 * PER_BLOCK + n], half_sem.at[n], half)

    def arrived(w, near, q, which, sem):
        ref = spot(w, near, q)
        remote(ref, ref, ici_send.at[0], sem.at[which * PER_BLOCK + w * PER_WEIGHT + q], side).wait_recv()

    def each(body):
        for w in range(3):

            @pl.loop(0, PER_WEIGHT)
            def _(q, w=w):
                body(w, q)

    @pl.when(end)
    def _():
        def first(w, q):
            to_side(w, 0, q, 0, own(w, q)).start()

        each(first)
        each(lambda w, q: to_core(w, 0, q, own(w, q)).start())

        def compute(w, q):
            k = kind[w]
            layer = q // PIECES
            cut = (layer, rows_of(0, heights[w], q, rows[w]))
            sources = (g_near[w].at[cut], w_old[w].at[layer, rows_of(at(1), heights[w], q, rows[w]), :], m_near[w].at[cut], v_near[w].at[cut])
            copies = [pltpu.make_async_copy(s, d[k], load_sem.at[i]) for i, (s, d) in enumerate(zip(sources, (g_in, w_in, m_in, v_in), strict=True))]
            for c in copies:
                c.start()
            for c in copies:
                c.wait()
            f = factor[0, 0]

            @pl.loop(0, rows[w] // GROUP)
            def _(i):
                part = pl.ds(pl.multiple_of(i * GROUP, GROUP), GROUP)
                g = g_in[k][part, :].astype(F32) * f
                old = w_in[k][part, :].astype(F32)
                m = 0.9 * m_in[k][part, :] + 0.1 * g
                v = 0.95 * v_in[k][part, :] + 0.05 * g * g
                out[k][part, :] = (old - 0.02 * (m * lax.rsqrt(v + 1e-8) + 0.1 * old)).astype(BF16)

            store = pltpu.make_async_copy(out[k], spot(w, 1, q), store_sem)
            pass_on = to_core(w, 1, q, out[k])
            store.start()
            pass_on.start()
            store.wait()
            pass_on.wait_send()

        each(compute)
        for which, near in enumerate((2, 3)):

            def hand_on(w, q, which=which, near=near):
                arrived(w, near, q, which, side_sem)
                to_core(w, near, q, spot(w, near, q)).start()

            each(hand_on)

        def finish(w, q):
            to_side(w, 0, q, 0, own(w, q)).wait_send()
            to_core(w, 0, q, own(w, q)).wait_send()
            to_core(w, 2, q, spot(w, 2, q)).wait_send()
            to_core(w, 3, q, spot(w, 3, q)).wait_send()

        each(finish)

    @pl.when(jnp.logical_not(end))
    def _():
        each(lambda w, q: to_half(w, 1, q, 0, own(w, q)).start())
        each(lambda w, q: to_core(w, 1, q, own(w, q)).start())

        def pass_both(w, q):
            arrived(w, 2, q, 0, half_sem)
            to_side(w, 2, q, 0, spot(w, 2, q)).start()
            to_core(w, 2, q, spot(w, 2, q)).start()
            arrived(w, 0, q, 0, side_sem)
            to_half(w, 0, q, 1, spot(w, 0, q)).start()
            to_core(w, 0, q, spot(w, 0, q)).start()

        each(pass_both)

        def pass_far(w, q):
            arrived(w, 3, q, 1, half_sem)
            to_side(w, 3, q, 1, spot(w, 3, q)).start()
            to_core(w, 3, q, spot(w, 3, q)).start()

        each(pass_far)

        def finish(w, q):
            to_half(w, 1, q, 0, own(w, q)).wait_send()
            to_half(w, 0, q, 1, spot(w, 0, q)).wait_send()
            to_side(w, 2, q, 0, spot(w, 2, q)).wait_send()
            to_side(w, 3, q, 1, spot(w, 3, q)).wait_send()
            to_core(w, 1, q, own(w, q)).wait_send()
            for near in (0, 2, 3):
                to_core(w, near, q, spot(w, near, q)).wait_send()

        each(finish)

    def last(w, q):
        for near in range(4):
            from_core(w, near, q)

    each(last)


def adamw(w, m, v, g):
    m = 0.9 * m + 0.1 * g
    v = 0.95 * v + 0.05 * g * g
    step = m * lax.rsqrt(v + 1e-8) + 0.1 * w
    return (w - 0.02 * step).astype(BF16), m, v


def solution(mesh):
    def step(*arrays):
        terms, weights, m, v = (arrays[i : i + 3] for i in (0, 3, 6, 9))
        heights = tuple(one.shape[1] for one in m)
        widths = tuple(one.shape[2] for one in m)
        block = [(2, h, c) for h, c in zip(heights, widths, strict=True)]
        big = [(h // PIECES, c) for h, c in zip(heights[1:], widths[1:], strict=True)]
        like = lambda lead, t: [jax.ShapeDtypeStruct((*lead, *b), t) for b in block]
        dma = pltpu.SemaphoreType.DMA
        outs = pl.pallas_call(
            functools.partial(reduce_kernel, heights),
            out_shape=(
                *like((), BF16), *like((), BF16), *like((), F32), *like((), F32), *like((3,), BF16), *like((2,), BF16), *like((4,), BF16),
                jax.ShapeDtypeStruct((8, GROUP, 128), F32),
            ),
            in_specs=[ANY] * 9,
            out_specs=(*[ANY] * 21, pl.BlockSpec(memory_space=pltpu.VMEM)),
            scratch_shapes=[
                *[pltpu.VMEM((SLOTS, *b), BF16) for b in big],
                *[pltpu.VMEM((SLOTS, *b), BF16) for b in big],
                *[pltpu.VMEM((2, 4, *b), BF16) for b in big],
                *[pltpu.VMEM((GROUP, b[1]), F32) for b in big],
                pltpu.VMEM((8, GROUP, 128), F32),
                dma((2, SLOTS)), dma((2, SLOTS)), dma((2, 4)), dma,
                dma((3 * PER_BLOCK,)), dma((2 * PER_BLOCK,)), dma((24,)), dma((24,)), dma((6,)), dma((6,)), dma((18,)), dma((18,)), dma((7,)), dma((7,)),
            ],
            compiler_params=pltpu.CompilerParams(has_side_effects=True),
            name="reduce",
        )(*terms, *m, *v)
        g, g_near, m_near, v_near = (outs[i : i + 3] for i in (0, 3, 6, 9))
        squares = jnp.sum(outs[21])
        count = 8 * sum(one.size for one in m)
        factor = jnp.minimum(1.0, 0.5 * lax.rsqrt(squares / count + 1e-30))
        me = lax.axis_index("dp")
        own = [lax.dynamic_slice_in_dim(w, me * h, h, 1).astype(F32) for w, h in zip(weights, heights, strict=True)]
        new = [adamw(w, m, v, g.astype(F32) * factor) for w, m, v, g in zip(own, m, v, g, strict=True)]
        whole = pl.pallas_call(
            functools.partial(gather_kernel, heights),
            out_shape=tuple(jax.ShapeDtypeStruct(w.shape, BF16) for w in weights),
            in_specs=[pl.BlockSpec(memory_space=pltpu.SMEM), *[ANY] * 15],
            out_specs=(ANY,) * 3,
            scratch_shapes=[
                *[pltpu.VMEM(b, BF16) for b in big], *[pltpu.VMEM(b, BF16) for b in big],
                *[pltpu.VMEM(b, F32) for b in big], *[pltpu.VMEM(b, F32) for b in big],
                *[pltpu.VMEM(b, BF16) for b in big],
                dma((4,)), dma, dma((4 * PER_BLOCK,)), dma((4 * PER_BLOCK,)), dma((2 * PER_BLOCK,)), dma((2 * PER_BLOCK,)), dma((4 * PER_BLOCK,)),
            ],
            compiler_params=pltpu.CompilerParams(has_side_effects=True),
            name="gather",
        )(factor.reshape(1, 1), *(one[0] for one in new), *weights, *g_near, *m_near, *v_near)
        whole = [lax.dynamic_update_slice_in_dim(w, one[0], me * h, 1) for w, one, h in zip(whole, new, heights, strict=True)]
        return (*whole, *(one[1] for one in new), *(one[2] for one in new))

    all_of, cut = P(None, None, None), P(None, "dp", None)
    return jax.shard_map(
        step,
        mesh=mesh,
        in_specs=(P(("rep", "dp"), None, None, None),) * 3 + (all_of,) * 3 + (cut,) * 6,
        out_specs=(P("rep", None, None),) * 3 + (P("rep", "dp", None),) * 6,
        check_vma=False,
    )
```

time: 1550 us -> 1210 us (0.78)
  waiting for transfers between devices: 1420 us -> 0 us
  Pallas kernels: 0 us -> 1100 us
    pallas_call x0 -> x2, Pallas kernels: none -> 1100 us  [the longest x1 664 us: step(): pl.pallas_call(functools.partial(reduce_kernel, heights), out_shape=(*lik...]
    reduce_scatter x3 -> x0, waiting for transfers between devices: 759 us -> none  [step(): lax.psum_scatter(t[0], 'dp', scatter_dimension=1, tiled=True)]
    all_gather x3 -> x0, waiting for transfers between devices: 655 us -> none  [step(): whole = [lax.all_gather(one[0], 'dp', axis=1, tiled=True) for one in new]]
    unnamed x19 -> x27, local copies, waits for them, and re-layouts: 55.6 us -> 57.9 us
    convert_element_type x3 -> x2, other arithmetic: 38.2 us -> 37.3 us  [adamw(): return ((w - 0.02 * step).astype(BF16), m, v)]
  transfers between devices with their start and end apart: 6 -> 0, of which waited for: 6 -> 0; matrix products, arithmetic and copies ran while one was open for 2% -> 0% of each run, Pallas kernels for 0% -> 0%
where the time goes in v1:
time: 1210 us
  Pallas kernels  1100 us (91%)
  local copies, waits for them, and re-layouts  63.7 us (5%)
  other arithmetic  38.7 us (3%)
    pallas_call x1, Pallas kernels, step(): pl.pallas_call(functools.partial(reduce_kernel, heights), out_shape=(*lik...  664 us
    pallas_call x1, Pallas kernels, step(): pl.pallas_call(functools.partial(gather_kernel, heights), out_shape=tuple...  441 us
    unnamed x27, local copies, waits for them, and re-layouts  57.9 us
    convert_element_type x2, other arithmetic, adamw(): return ((w - 0.02 * step).astype(BF16), m, v)  37.3 us

profile of v1, /device:TPU:0, one launch (start us, length us, event | category | flops | bytes accessed | tf_op | source)
XLA Modules:
  0.0 1208.2 jit_solution(8825380113218069593)
XLA Ops:
  0.6 663.6 %reduce.1 = (bf16[2,192,4224]{2,1,0:T(8,128)(2,1)}, bf16[2,192,4224]{2,1,0:T(8,128)(2,1)}, bf16[2,528,1536]{2,1,0:T(8,128)(2,1)}, bf16[2,192,4224]{2,1,0:T(8,128...) custom-call(bf16[1,2,1536,4224]{3,2,1,0:T(8,128)(2,1)} %refs_0_.1, ...), custom_call_target="tpu_custom_call" | custom-call | tf_op jit(solution)/shard_map/reduce/pallas_call | solution.py:434
  664.3 1.5 reduce_sum.9
  666.4 0.0 copy-start.3
  666.4 0.0 copy-start.4
  666.4 14.0 %fusion.8 = (bf16[2,528,1536]{2,1,0:T(8,128)(2,1)}, f32[2,528,1536]{2,1,0:T(8,128)}, f32[2,528,1536]{2,1,0:T(8,128)}) fusion(bf16[2,4224,1536]{2,1,0:T(8,128)(2,1)} %refs_6_.3, s32[]{:T(128)S(6)} %select_n.5, f32[]{:T(128)} %min_shard_map.3, bf16[2,528,1536]{2,1,0:T(8,128)(2,1)} %get-tuple-element.28, f32[2,528,1536]{2,1,0:T(8,128)} %refs_8_.1, ...), kind=kLoop, calls=%fused_computation.17 | loop fusion | flops 27574272 | bytes 35684360 | tf_op jit(solution)/shard_map/convert_element_type | solution.py:422
  680.4 0.0 copy-done.3
  680.4 1.1 copy-done.4
  681.6 23.2 %fusion.2 = (bf16[2,192,4224]{2,1,0:T(8,128)(2,1)}, f32[2,192,4224]{2,1,0:T(8,128)}, f32[2,192,4224]{2,1,0:T(8,128)}, bf16[2,192,4224]{2,1,0:T(8,128)(2,1)}, f32...) fusion(bf16[2,1536,4224]{2,1,0:T(8,128)(2,1)} %refs_4_.3, s32[]{:T(128)S(6)} %select_n.4, f32[]{:T(128)} %min_shard_map.3, ...), kind=kLoop, calls=%fused_computation.11 | loop fusion | flops 55148544 | bytes 71368712 | tf_op jit(solution)/shard_map/convert_element_type | solution.py:422
  704.8 0.0 copy-start.2
  704.8 440.7 %gather.1 = (bf16[2,1536,4224]{2,1,0:T(8,128)(2,1)}, bf16[2,1536,4224]{2,1,0:T(8,128)(2,1)}, bf16[2,4224,1536]{2,1,0:T(8,128)(2,1)}) custom-call(f32[1,1]{1,0:T(1,128)} %bitcast.refs_0_, bf16[2,192,4224]{2,1,0:T(8,128)(2,1)} %get-tuple-element.47.refs_1_, bf16[2,192,4224]{2,1,0:T(8,128)(2,1)} %get-tuple-element.50.refs_2_, ...), custom_call_target="tpu_custom_call" | custom-call | tf_op jit(solution)/shard_map/gather/pallas_call | solution.py:461
  1145.5 0.0 copy-start.1
  1145.5 0.0 copy-done.2
  1145.5 0.0 copy-start
  1145.5 1.9 constant_dynamic-update-slice_fusion.2
  1147.4 1.2 copy-done.1
  1148.6 1.9 constant_dynamic-update-slice_fusion.1
  1150.5 0.0 copy-done
  1150.5 2.0 constant_dynamic-update-slice_fusion
  1152.5 0.0 slice-start
  1152.5 0.0 slice-start.1
  1152.5 0.0 slice-start.2
  1152.5 0.0 slice-start.3
  1152.5 23.9 %copy.27 = bf16[2,1536,4224]{2,1,0:T(8,128)(2,1)} copy(bf16[2,1536,4224]{2,1,0:T(8,128)(2,1)} %constant_dynamic-update-slice_fusion.2) | data formatting | bytes 51904512
  1176.4 0.0 slice-start.4
  1176.4 0.0 slice-start.5
  1176.4 0.0 slice-start.6
  1176.4 22.6 %copy.28 = bf16[2,1536,4224]{2,1,0:T(8,128)(2,1)} copy(bf16[2,1536,4224]{2,1,0:T(8,128)(2,1)} %constant_dynamic-update-slice_fusion.1) | data formatting | bytes 51904512
  1198.9 0.0 slice-done
  1198.9 0.0 slice-done.1
  1198.9 0.0 slice-done.2
  1198.9 0.0 slice-done.3
  1199.0 0.0 slice-done.4
  1199.0 0.0 slice-done.5
  1199.0 0.0 slice-done.6
  1199.0 9.2 copy.29
  (1 shorter events, 0.0 us)
Async XLA Ops:
  666.4 14.0 %copy-start.3 = (f32[2,192,4224]{2,1,0:T(8,128)S(1)}, f32[2,192,4224]{2,1,0:T(8,128)}, u32[]{:S(2)}) copy-start(f32[2,192,4224]{2,1,0:T(8,128)} %refs_3_.1) | copy-start | bytes 19464196
  666.4 15.1 %copy-start.4 = (bf16[2,192,4224]{2,1,0:T(8,128)(2,1)S(1)}, bf16[2,192,4224]{2,1,0:T(8,128)(2,1)}, u32[]{:S(2)}) copy-start(bf16[2,192,4224]{2,1,0:T(8,128)(2,1)} %get-tuple-element.26) | copy-start | bytes 9732100
  704.8 440.7 %copy-start.2 = (bf16[2,192,4224]{2,1,0:T(8,128)(2,1)S(1)}, bf16[2,192,4224]{2,1,0:T(8,128)(2,1)}, u32[]{:S(2)}) copy-start(bf16[2,192,4224]{2,1,0:T(8,128)(2,1)} %get-tuple-element.47.refs_1_) | copy-start | bytes 9732100
  1145.5 3.1 copy-start.1
  1145.5 5.0 copy-start
  1152.5 46.4 %slice-start = ((s8[25952256]{0:T(1024)(128)(4,1)}), s8[4194304]{0:T(1024)(128)(4,1)S(1)}, s32[]{:S(2)}) async-start(s8[25952256]{0:T(1024)(128)(4,1)} %bitcast.1), calls=%async_computation | async-start | bytes 8388608
  1152.5 46.4 %slice-start.1 = ((s8[25952256]{0:T(1024)(128)(4,1)}), s8[4194304]{0:T(1024)(128)(4,1)S(1)}, s32[]{:S(2)}) async-start(s8[25952256]{0:T(1024)(128)(4,1)} %bitcast.1), calls=%async_computation.1 | async-start | bytes 8388608
  1152.5 46.4 %slice-start.2 = ((s8[25952256]{0:T(1024)(128)(4,1)}), s8[4194304]{0:T(1024)(128)(4,1)S(1)}, s32[]{:S(2)}) async-start(s8[25952256]{0:T(1024)(128)(4,1)} %bitcast.1), calls=%async_computation.2 | async-start | bytes 8388608
  1152.5 46.4 %slice-start.3 = ((s8[25952256]{0:T(1024)(128)(4,1)}), s8[4194304]{0:T(1024)(128)(4,1)S(1)}, s32[]{:S(2)}) async-start(s8[25952256]{0:T(1024)(128)(4,1)} %bitcast.1), calls=%async_computation.3 | async-start | bytes 8388608
  1176.4 22.6 %slice-start.4 = ((s8[25952256]{0:T(1024)(128)(4,1)}), s8[4194304]{0:T(1024)(128)(4,1)S(1)}, s32[]{:S(2)}) async-start(s8[25952256]{0:T(1024)(128)(4,1)} %bitcast.1), calls=%async_computation.4 | async-start | bytes 8388608
  1176.4 22.6 %slice-start.5 = ((s8[25952256]{0:T(1024)(128)(4,1)}), s8[4194304]{0:T(1024)(128)(4,1)S(1)}, s32[]{:S(2)}) async-start(s8[25952256]{0:T(1024)(128)(4,1)} %bitcast.1), calls=%async_computation.5 | async-start | bytes 8388608
  1176.4 22.6 %slice-start.6 = ((s8[25952256]{0:T(1024)(128)(4,1)}), s8[786432]{0:T(1024)(128)(4,1)S(1)}, s32[]{:S(2)}) async-start(s8[25952256]{0:T(1024)(128)(4,1)} %bitcast.1), calls=%async_computation.6 | async-start | bytes 1572864
